TPU v7x, 32 devices: a whole 2x2x4 slice. The times are simulated.
32 devices in a mesh: chain: 4 (over y, core), cols: 8 (over z, x).
Axes of the slice: x: 2, y: 2, z: 4, core: 2. Of those that a mesh axis runs over, the one named last changes fastest.
Arguments:
- factor: float32 [4608, 4608], P(('chain', 'cols')), may hold values from -2 to 2, as said below
- right_side: float32 [4608, 1024], P('chain', 'cols'), may hold values from -6 to 6
- occ_order: int32 [16], replicated, may hold values from 0 to 15, each once
- cabs_order: int32 [64], replicated, may hold values from 0 to 63, each once
Outputs:
- fitted: float32 [16, 64, 4608], P('cols', None, 'chain')
Inputs may be any that keep to these rules, and one draw needn't show every extreme that they name: factor is lower triangular: zero above the diagonal, its diagonal between 1 and 2.
All inputs are finite; a program needn't handle non-finite values.
Results may differ from a plain program's by a relative error of at most 0.00017.
Values sent between devices are 32-bit elements; how exact they have to be, the bound alone decides.
A program may use at most 128 MiB of HBM per device.

v0:
```python
import jax
import jax.numpy as jnp
from jax import lax
from jax.sharding import PartitionSpec as P


def from_root(value, axis, source):
    kept = jnp.where(lax.axis_index(axis) == source, value, 0).astype(value.dtype)
    return lax.psum(kept, axis)


def product(left, right):
    return jnp.dot(left, right, precision=lax.Precision.HIGHEST, preferred_element_type=jnp.float32)


def per_device(factor, right_side, occ_order, cabs_order):
    chain_size = lax.axis_size("chain")
    position = lax.axis_index("chain")
    factor_row = lax.all_gather(factor, "cols", axis=0, tiled=True)
    aux_rows = factor_row.shape[0]
    diag_block = lax.dynamic_slice_in_dim(factor_row, position * aux_rows, aux_rows, 1)
    identity = jnp.eye(aux_rows, dtype=jnp.float32)
    inverse = jax.scipy.linalg.solve_triangular(diag_block, identity, lower=True)

    def settle(residual):
        return product(inverse, residual)

    def blank(residual):
        return jnp.zeros_like(residual)

    residual = right_side
    solution = jnp.zeros_like(right_side)
    for section in range(chain_size):
        solved = lax.cond(position == section, settle, blank, residual)
        solution = solution + solved
        if section + 1 < chain_size:
            arrived = from_root(solved, "chain", section)
            coupling = factor_row[:, section * aux_rows : (section + 1) * aux_rows]

            def lower_block(current, arrived=arrived, coupling=coupling):
                return current - product(coupling, arrived)

            def keep_block(current):
                return current

            residual = lax.cond(position > section, lower_block, keep_block, residual)
    occ_total = occ_order.shape[0]
    cabs_local = right_side.shape[1] // occ_total
    cols_size = lax.axis_size("cols")
    occ_local = occ_total // cols_size
    grid = solution.reshape(aux_rows, cabs_local, occ_total)
    grid = jnp.take(grid, occ_order, axis=2)
    grid = grid.reshape(aux_rows, cabs_local, cols_size, occ_local)
    grid = jnp.transpose(grid, (2, 3, 1, 0))
    moved = jnp.take(
        lax.all_to_all(grid, "cols", split_axis=0, concat_axis=2, tiled=True), cabs_order, axis=2
    )
    return moved.reshape(occ_local, moved.shape[2], aux_rows)


def solution(mesh):
    in_specs = (P(("chain", "cols"), None), P("chain", "cols"), P(), P())
    out_specs = P("cols", None, "chain")
    return jax.shard_map(
        per_device, mesh=mesh, in_specs=in_specs, out_specs=out_specs, check_vma=False
    )
```

profile of v0, /device:TPU:5, one launch (start us, length us, event | category | flops | bytes accessed | tf_op | source)
XLA Modules:
  0.0 739.5 jit_solution(7682201106156119193)
XLA Ops:
  6.5 1.1 copy.72
  7.7 0.4 iota_compare_fusion
  8.1 2.7 fusion.27
  10.8 405.7 %all-gather.2.cloned.1.call-done = f32[1152,4608]{1,0:T(8,128)} async-done(((f32[144,4608]{1,0:T(8,128)}), f32[1152,4608]{1,0:T(8,128)}) %all-gather.2.cloned.1.call-update) | async-done | bytes 21233680 | tf_op jit(solution)/shard_map/all_gather | solution.py:19
  416.6 5.2 dynamic-slice_select_fusion
  421.8 25.2 %while.1 = (s32[]{:T(128)}, f32[1152,1152]{1,0:T(8,128)}, s32[9,2]{0,1:T(2,128)S(1)}, f32[9,128,128]{2,1,0:T(8,128)S(1)}, s32[]{:T(128)}) while((s32[]{:T(128)}, f32[1152,1152]{1,0:T(8,128)}, s32[9,2]{0,1:T(2,128)S(1)}, f32[9,128,128]{2,1,0:T(8,128)S(1)}, s32[]{:T(128)}) %tuple.105), condition=%wide.while_cond, body=%wide.while_body.sunk | while | flops 2 | bytes 131181 | solution.py:23
  421.8 0.5 fusion.82
  422.4 2.2 bitcast_dynamic-update-slice_fusion.2
  424.6 0.5 fusion.82
  425.2 2.2 bitcast_dynamic-update-slice_fusion.2
  427.5 0.5 fusion.82
  428.0 2.2 bitcast_dynamic-update-slice_fusion.2
  430.3 0.5 fusion.82
  430.8 2.2 bitcast_dynamic-update-slice_fusion.2
  433.1 0.5 fusion.82
  433.6 2.2 bitcast_dynamic-update-slice_fusion.2
  435.9 0.5 fusion.82
  436.4 2.2 bitcast_dynamic-update-slice_fusion.2
  438.7 0.5 fusion.82
  439.2 2.2 bitcast_dynamic-update-slice_fusion.2
  441.5 0.5 fusion.82
  442.1 2.2 bitcast_dynamic-update-slice_fusion.2
  444.3 0.5 fusion.82
  444.9 2.1 bitcast_dynamic-update-slice_fusion.2
  447.0 88.9 %custom-call.4 = f32[9,128,128]{1,2,0:T(8,128)S(1)} custom-call(f32[9,128,128]{2,1,0:T(8,128)S(1)} %get-tuple-element.90), custom_call_target="InvertDiagBlocksLowerTriangular" | custom-call | tf_op jit(solution)/shard_map/jit(_solve_triangular)/triangular_solve | solution.py:23
  535.9 0.7 constant_dynamic-update-slice_fusion.25
  536.6 2.1 convolution_subtract_fusion.7
  538.7 0.9 constant_dynamic-update-slice_fusion.24
  539.6 1.7 convolution_subtract_fusion.6
  541.3 0.8 constant_dynamic-update-slice_fusion.23
  542.1 2.3 convolution_subtract_fusion.2
  544.4 0.9 constant_dynamic-update-slice_fusion.22
  545.3 2.4 convolution_subtract_fusion.5
  547.7 0.8 constant_dynamic-update-slice_fusion.21
  548.5 3.0 convolution_subtract_fusion
  551.5 0.7 constant_dynamic-update-slice_fusion.20
  552.2 3.4 convolution_subtract_fusion.1
  555.6 0.7 constant_dynamic-update-slice_fusion.19
  556.3 3.7 convolution_subtract_fusion.4
  560.0 0.7 constant_dynamic-update-slice_fusion.18
  560.7 3.9 convolution_subtract_fusion.3
  564.6 0.7 convolution_dynamic-update-slice_fusion
  565.3 2.3 copy-done
  567.9 0.9 broadcast_select_fusion.2
  568.8 35.9 %all-reduce.4.cloned.1.call-done = f32[1152,128]{1,0:T(8,128)} async-done(((f32[1152,128]{1,0:T(8,128)}), f32[1152,128]{1,0:T(8,128)}) %all-reduce.4.cloned.1.call-update) | async-done | bytes 589840 | tf_op jit(solution)/shard_map/psum | solution.py:9
  604.7 6.4 conditional.8
  604.7 6.4 fusion.2
  611.2 0.9 broadcast_select_fusion.1
  612.3 38.6 %all-reduce.6.cloned.1.call-done = f32[1152,128]{1,0:T(8,128)} async-done(((f32[1152,128]{1,0:T(8,128)}), f32[1152,128]{1,0:T(8,128)}) %all-reduce.6.cloned.1.call-update) | async-done | bytes 589840 | tf_op jit(solution)/shard_map/psum | solution.py:9
  650.9 6.4 conditional.10
  650.9 6.4 fusion.7
  657.4 0.9 broadcast_select_fusion
  659.0 39.4 %all-reduce.8.cloned.1.call-done = f32[1152,128]{1,0:T(8,128)} async-done(((f32[1152,128]{1,0:T(8,128)}), f32[1152,128]{1,0:T(8,128)}) %all-reduce.8.cloned.1.call-update) | async-done | bytes 589840 | tf_op jit(solution)/shard_map/psum | solution.py:9
  698.4 6.7 conditional.12
  698.6 6.4 fusion.12
  705.0 7.4 %conditional.13 = (f32[1152,128]{0,1:T(8,128)S(1)}) conditional(s32[]{:T(128)} %convert_element_type.48, () %tuple.55, (f32[1152,1152]{1,0:T(8,128)}, f32[1152,128]{1,0:T(8,128)S(1)}) %tuple.132), branch_computations={%region_15.16_spmd, %region_16.17_spmd} | conditional | flops 2038431744 | bytes 6488072 | solution.py:34
  705.0 7.4 %fusion.55 = f32[1152,128]{0,1:T(8,128)S(1)} fusion(f32[1152,1152]{1,0:T(8,128)} %get-tuple-element.79, f32[1152,128]{1,0:T(8,128)S(1)} %get-tuple-element.80), kind=kOutput, calls=%fused_computation.122 | convolution fusion | flops 2038431744 | bytes 6488064 | tf_op jit(solution)/shard_map/cond | solution.py:34
  712.8 0.6 gather_fusion
  713.4 0.9 select_bitcast_fusion.1
  714.3 5.5 all-to-all-start
  719.8 9.8 %all-to-all-done = f32[8,2,8,1152]{3,2,1,0:T(8,128)S(1)} async-done(((f32[8,2,8,1152]{3,2,1,0:T(8,128)}), f32[8,2,8,1152]{3,2,1,0:T(8,128)S(1)}, u32[]{:S(2)}, u32[]{:S(2)}) %all-to-all-start) | async-done | bytes 589856 | tf_op jit(solution)/shard_map/all_to_all | solution.py:56
  729.7 0.5 copy.11
  730.2 1.2 gather_fusion.1
  731.7 0.9 copy.12
  (46 shorter events, 2.9 us)
Async XLA Ops:
  6.5 410.0 %all-gather.2.cloned.1.call-start = ((), (), s32[]{:S(2)}) async-start(), calls=%async_computation.1 | async-start | bytes 23887872 | tf_op jit(solution)/shard_map/all_gather | solution.py:19
  7.6 597.1 %all-reduce.4.cloned.1.call-start = ((), (), s32[]{:S(2)}) async-start(), calls=%async_computation.2 | async-start | bytes 1179648 | tf_op jit(solution)/shard_map/psum | solution.py:9
  535.9 3.6 copy-start.1
  565.3 2.3 copy-start
  568.8 82.1 %all-reduce.6.cloned.1.call-start = ((), (), s32[]{:S(2)}) async-start(), calls=%async_computation.3 | async-start | bytes 1179648 | tf_op jit(solution)/shard_map/psum | solution.py:9
  611.1 1.0 copy-start.2
  612.1 86.2 %all-reduce.8.cloned.1.call-start = ((), (), s32[]{:S(2)}) async-start(), calls=%async_computation.4 | async-start | bytes 1179648 | tf_op jit(solution)/shard_map/psum | solution.py:9
  657.3 1.0 copy-start.3
  714.3 15.3 %all-to-all-start = ((f32[8,2,8,1152]{3,2,1,0:T(8,128)}), f32[8,2,8,1152]{3,2,1,0:T(8,128)S(1)}, u32[]{:S(2)}, u32[]{:S(2)}) async-start(f32[8,2,8,1152]{3,2,1,0:T(8,128)} %select_bitcast_fusion.1), calls=%async_computation | async-start | bytes 1179648 | tf_op jit(solution)/shard_map/all_to_all | solution.py:56
Sparse Core Ops, SparseCore 0:
  8.9 407.6 all-gather.1
  568.9 35.8 all-reduce.3
  612.2 38.5 all-reduce.5
  658.4 39.9 all-reduce.7
where the time goes:
time: 744 us; the launch traced here: 740 us
  waiting for transfers between devices  529 us (71%)
  other arithmetic  101 us (14%)
  matrix products  55.8 us (8%)
  local copies, waits for them, and re-layouts  32.7 us (4%)
  between operations  13.9 us (2%)
    all_gather x1, waiting for transfers between devices, per_device(): factor_row = lax.all_gather(factor, 'cols', axis=0, tiled=True)  406 us
    psum x3, waiting for transfers between devices, from_root(): return lax.psum(kept, axis)  114 us
    another operation x3, other arithmetic, per_device(): jax.scipy.linalg.solve_triangular(diag_block, identity, lower=True)  94.1 us
    another operation x17, matrix products, per_device(): jax.scipy.linalg.solve_triangular(diag_block, identity, lower=True)  29.2 us
    another operation x30, local copies, waits for them, and re-layouts  25.2 us
    dot_general x3, matrix products, product(): jnp.dot(left, right, precision=lax.Precision.HIGHEST, preferred_element_t...  19.2 us
  transfers between devices with their start and end apart: 5, of which 5 were waited for; matrix products, arithmetic and copies ran while one was open for 1% of the time, Pallas kernels for 0%

commit v1 on v0

--- a/solution.py
+++ b/solution.py
@@ -6,7 +6,7 @@
 
 def from_root(value, axis, source):
     kept = jnp.where(lax.axis_index(axis) == source, value, 0).astype(value.dtype)
-    return lax.psum(kept, axis)
+    return jnp.sum(lax.all_gather(kept, axis), axis=0)
 
 
 def product(left, right):

time: 744 us -> 728 us (0.978)
  waiting for transfers between devices: 529 us -> 504 us
    psum x3 -> x0, waiting for transfers between devices: 114 us -> none  [from_root(): return lax.psum(kept, axis)]
    all_gather x0 -> x3, waiting for transfers between devices: none -> 87 us  [from_root(): return jnp.sum(lax.all_gather(kept, axis), axis=0)]
    another operation x30 -> x31, local copies, waits for them, and re-layouts: 25.2 us -> 26.7 us
where the time goes in v1:
time: 728 us; the launch traced here: 724 us
  waiting for transfers between devices  504 us (69%)
  other arithmetic  106 us (15%)
  matrix products  60.4 us (8%)
  local copies, waits for them, and re-layouts  33.2 us (5%)
  between operations  13.7 us (2%)
    all_gather x1, waiting for transfers between devices, per_device(): factor_row = lax.all_gather(factor, 'cols', axis=0, tiled=True)  406 us
    another operation x3, other arithmetic, per_device(): jax.scipy.linalg.solve_triangular(diag_block, identity, lower=True)  93.8 us
    all_gather x3, waiting for transfers between devices, from_root(): return jnp.sum(lax.all_gather(kept, axis), axis=0)  87 us
    another operation x17, matrix products, per_device(): jax.scipy.linalg.solve_triangular(diag_block, identity, lower=True)  29.2 us
    another operation x31, local copies, waits for them, and re-layouts  26.7 us
    dot_general x3, matrix products, product(): jnp.dot(left, right, precision=lax.Precision.HIGHEST, preferred_element_t...  23.6 us
  transfers between devices with their start and end apart: 5, of which 5 were waited for; matrix products, arithmetic and copies ran while one was open for 1% of the time, Pallas kernels for 0%

profile of v1, /device:TPU:5, one launch (start us, length us, event | category | flops | bytes accessed | tf_op | source)
XLA Modules:
  0.0 724.0 jit_solution(8520998087109370749)
XLA Ops:
  6.5 0.7 all-gather.8.cloned.1.call-update
  7.7 2.7 fusion.36
  10.5 406.1 %all-gather.8.cloned.1.call-done = f32[1152,4608]{1,0:T(8,128)} async-done(((f32[144,4608]{1,0:T(8,128)}), f32[1152,4608]{1,0:T(8,128)}) %all-gather.8.cloned.1.call-update) | async-done | bytes 21233680 | tf_op jit(solution)/shard_map/all_gather | solution.py:19
  416.6 5.2 dynamic-slice_select_fusion
  421.8 26.5 %while.1 = (s32[]{:T(128)}, f32[1152,1152]{1,0:T(8,128)}, s32[9,2]{0,1:T(2,128)S(1)}, f32[9,128,128]{2,1,0:T(8,128)S(1)}, s32[]{:T(128)}) while((s32[]{:T(128)}, f32[1152,1152]{1,0:T(8,128)}, s32[9,2]{0,1:T(2,128)S(1)}, f32[9,128,128]{2,1,0:T(8,128)S(1)}, s32[]{:T(128)}) %tuple.114), condition=%wide.while_cond, body=%wide.while_body.sunk | while | flops 2 | bytes 131181 | solution.py:23
  422.4 2.3 bitcast_dynamic-update-slice_fusion.2
  424.8 0.6 fusion.91
  425.4 2.3 bitcast_dynamic-update-slice_fusion.2
  427.7 0.6 fusion.91
  428.3 2.3 bitcast_dynamic-update-slice_fusion.2
  430.7 0.6 fusion.91
  431.3 2.3 bitcast_dynamic-update-slice_fusion.2
  433.6 0.6 fusion.91
  434.2 2.3 bitcast_dynamic-update-slice_fusion.2
  436.6 0.6 fusion.91
  437.2 2.3 bitcast_dynamic-update-slice_fusion.2
  439.5 0.6 fusion.91
  440.1 2.3 bitcast_dynamic-update-slice_fusion.2
  442.5 0.6 fusion.91
  443.1 2.3 bitcast_dynamic-update-slice_fusion.2
  445.4 0.6 fusion.91
  446.0 2.2 bitcast_dynamic-update-slice_fusion.2
  448.3 88.6 %custom-call.4 = f32[9,128,128]{1,2,0:T(8,128)S(1)} custom-call(f32[9,128,128]{2,1,0:T(8,128)S(1)} %get-tuple-element.96), custom_call_target="InvertDiagBlocksLowerTriangular" | custom-call | tf_op jit(solution)/shard_map/jit(_solve_triangular)/triangular_solve | solution.py:23
  536.9 0.7 constant_dynamic-update-slice_fusion.25
  537.5 2.1 convolution_subtract_fusion.7
  539.6 0.8 constant_dynamic-update-slice_fusion.24
  540.5 1.7 convolution_subtract_fusion.6
  542.2 0.8 constant_dynamic-update-slice_fusion.23
  543.0 2.3 convolution_subtract_fusion.2
  545.3 0.9 constant_dynamic-update-slice_fusion.22
  546.2 2.4 convolution_subtract_fusion.5
  548.6 0.8 constant_dynamic-update-slice_fusion.21
  549.4 3.0 convolution_subtract_fusion
  552.4 0.7 constant_dynamic-update-slice_fusion.20
  553.1 3.4 convolution_subtract_fusion.1
  556.5 0.7 constant_dynamic-update-slice_fusion.19
  557.2 3.7 convolution_subtract_fusion.4
  560.9 0.7 constant_dynamic-update-slice_fusion.18
  561.6 3.9 convolution_subtract_fusion.3
  565.5 0.7 convolution_dynamic-update-slice_fusion
  566.2 2.3 copy-done
  569.0 0.9 broadcast_select_fusion.2
  570.0 27.1 %all-gather.10.cloned.1.call-done = f32[4608,128]{1,0:T(8,128)} async-done(((f32[1152,128]{1,0:T(8,128)}), f32[4608,128]{1,0:T(8,128)}) %all-gather.10.cloned.1.call-update) | async-done | bytes 2359312 | tf_op jit(solution)/shard_map/all_gather | solution.py:9
  597.1 9.8 %conditional.8 = (f32[1152,128]{0,1:T(8,128)S(1)}) conditional(s32[]{:T(128)} %convert_element_type.45, (f32[1152,128]{1,0:T(8,128)S(1)}) %tuple.143, (f32[1152,4608]{1,0:T(8,128)}, f32[4,1152,128]{2,1,0:T(8,128)}, f32[1152,128]{1,0:T(8,128)S(1)}, f32[]{:T(128)}) %tuple.146), branch_computations={%region_3.4_spmd, %region_4.5_spmd} | conditional | flops 2039021568 | bytes 11206668 | solution.py:46
  597.3 1.9 reduce_sum.30
  599.1 7.8 %fusion.5 = f32[1152,128]{0,1:T(8,128)S(1)} fusion(f32[1152,128]{0,1:T(8,128)S(1)} %copy.11, f32[1152,128]{1,0:T(8,128)S(1)} %reduce_sum.30, f32[1152,4608]{1,0:T(8,128)} %get-tuple-element.83), kind=kOutput, calls=%fused_computation.5 | convolution fusion | flops 2038579200 | bytes 7077888 | tf_op jit(solution)/shard_map/cond/branch_1_fun/dot_general | solution.py:13
  607.0 0.9 broadcast_select_fusion.1
  607.9 30.3 %all-gather.12.cloned.1.call-done = f32[4608,128]{1,0:T(8,128)} async-done(((f32[1152,128]{1,0:T(8,128)}), f32[4608,128]{1,0:T(8,128)}) %all-gather.12.cloned.1.call-update) | async-done | bytes 2359312 | tf_op jit(solution)/shard_map/all_gather | solution.py:9
  638.2 10.0 %conditional.10 = (f32[1152,128]{0,1:T(8,128)S(1)}) conditional(s32[]{:T(128)} %convert_element_type.47, f32[1152,128]{0,1:T(8,128)S(1)} %get-tuple-element.217, (f32[1152,4608]{1,0:T(8,128)}, f32[4,1152,128]{2,1,0:T(8,128)}, f32[1152,128]{0,1:T(8,128)S(1)}, f32[]{:T(128)}) %tuple.147), branch_computations={%region_8.9_spmd, %region_9.10_spmd} | conditional | flops 2039021568 | bytes 10027020 | solution.py:46
  638.4 1.9 reduce_sum.31
  640.2 7.9 %fusion.13 = f32[1152,128]{0,1:T(8,128)S(1)} fusion(f32[1152,128]{0,1:T(8,128)S(1)} %get-tuple-element.73, f32[1152,128]{1,0:T(8,128)S(1)} %reduce_sum.31, f32[1152,4608]{1,0:T(8,128)} %get-tuple-element.86), kind=kOutput, calls=%fused_computation.9 | convolution fusion | flops 2038579200 | bytes 7077888 | tf_op jit(solution)/shard_map/cond/branch_1_fun/dot_general | solution.py:13
  648.3 0.9 broadcast_select_fusion
  650.0 29.6 %all-gather.14.cloned.1.call-done = f32[4608,128]{1,0:T(8,128)} async-done(((f32[1152,128]{1,0:T(8,128)}), f32[4608,128]{1,0:T(8,128)}) %all-gather.14.cloned.1.call-update) | async-done | bytes 2359312 | tf_op jit(solution)/shard_map/all_gather | solution.py:9
  679.6 10.0 %conditional.12 = (f32[1152,128]{0,1:T(8,128)S(1)}) conditional(s32[]{:T(128)} %convert_element_type.49, f32[1152,128]{0,1:T(8,128)S(1)} %get-tuple-element.219, (f32[4,1152,128]{2,1,0:T(8,128)}, f32[1152,4608]{1,0:T(8,128)}, f32[1152,128]{0,1:T(8,128)S(1)}) %tuple.145), branch_computations={%region_12.13_spmd, %region_13.15_spmd} | conditional | flops 2039021568 | bytes 10027020 | solution.py:46
  679.8 1.9 reduce_sum.25
  681.7 7.9 %fusion.21 = f32[1152,128]{0,1:T(8,128)S(1)} fusion(f32[1152,128]{0,1:T(8,128)S(1)} %get-tuple-element.78, f32[1152,128]{1,0:T(8,128)S(1)} %reduce_sum.25, f32[1152,4608]{1,0:T(8,128)} %get-tuple-element.80), kind=kOutput, calls=%fused_computation.13 | convolution fusion | flops 2038579200 | bytes 7077888 | tf_op jit(solution)/shard_map/cond/branch_1_fun/dot_general | solution.py:13
  689.6 7.6 %conditional.13 = (f32[1152,128]{0,1:T(8,128)S(1)}) conditional(s32[]{:T(128)} %convert_element_type.48, () %tuple.55, (f32[1152,1152]{1,0:T(8,128)}, f32[1152,128]{0,1:T(8,128)S(1)}) %tuple.141), branch_computations={%region_15.16_spmd, %region_16.17_spmd} | conditional | flops 2038431744 | bytes 6488072 | solution.py:34
  689.7 7.6 %fusion.64 = f32[1152,128]{0,1:T(8,128)S(1)} fusion(f32[1152,1152]{1,0:T(8,128)} %get-tuple-element.81, f32[1152,128]{0,1:T(8,128)S(1)} %get-tuple-element.116), kind=kOutput, calls=%fused_computation.125 | convolution fusion | flops 2038431744 | bytes 6488064 | tf_op jit(solution)/shard_map/cond | solution.py:34
  697.6 0.6 gather_fusion
  698.2 0.9 select_bitcast_fusion.1
  699.1 5.4 all-to-all-start
  704.5 9.8 %all-to-all-done = f32[8,2,8,1152]{3,2,1,0:T(8,128)S(1)} async-done(((f32[8,2,8,1152]{3,2,1,0:T(8,128)}), f32[8,2,8,1152]{3,2,1,0:T(8,128)S(1)}, u32[]{:S(2)}, u32[]{:S(2)}) %all-to-all-start) | async-done | bytes 589856 | tf_op jit(solution)/shard_map/all_to_all | solution.py:56
  714.9 1.2 gather_fusion.1
  716.4 0.9 copy.22
  (51 shorter events, 4.7 us)
Async XLA Ops:
  6.5 410.0 %all-gather.8.cloned.1.call-start = ((), (), s32[]{:S(2)}) async-start(), calls=%async_computation.1 | async-start | bytes 23887872 | tf_op jit(solution)/shard_map/all_gather | solution.py:19
  7.3 589.8 %all-gather.10.cloned.1.call-start = ((), (), s32[]{:S(2)}) async-start(), calls=%async_computation.2 | async-start | bytes 2949120 | tf_op jit(solution)/shard_map/all_gather | solution.py:9
  536.8 3.6 copy-start.1
  560.9 5.3 copy-start.2
  566.2 2.3 copy-start
  569.9 68.3 %all-gather.12.cloned.1.call-start = ((), (), s32[]{:S(2)}) async-start(), calls=%async_computation.3 | async-start | bytes 2949120 | tf_op jit(solution)/shard_map/all_gather | solution.py:9
  607.9 71.8 %all-gather.14.cloned.1.call-start = ((), (), s32[]{:S(2)}) async-start(), calls=%async_computation.4 | async-start | bytes 2949120 | tf_op jit(solution)/shard_map/all_gather | solution.py:9
  648.2 1.0 copy-start.3
  648.2 1.1 copy-start.4
  699.1 15.3 %all-to-all-start = ((f32[8,2,8,1152]{3,2,1,0:T(8,128)}), f32[8,2,8,1152]{3,2,1,0:T(8,128)S(1)}, u32[]{:S(2)}, u32[]{:S(2)}) async-start(f32[8,2,8,1152]{3,2,1,0:T(8,128)} %select_bitcast_fusion.1), calls=%async_computation | async-start | bytes 1179648 | tf_op jit(solution)/shard_map/all_to_all | solution.py:56
Sparse Core Ops, SparseCore 0:
  8.9 407.6 all-gather.7
  570.0 26.9 all-gather.9
  608.0 30.1 all-gather.11
  649.3 30.3 all-gather.13
